TPU v7x, 512 devices: a whole 4x4x16 slice. The times are simulated.
512 devices in a mesh: mem: 128 (over x, y, z_lo), slab: 4 (over z_hi, core).
Axes of the slice: x: 4, y: 4, z: 16 (z_hi: 2, z_lo: 8; z = z_hi * 8 + z_lo), core: 2. Of those that a mesh axis runs over, the one named last changes fastest.
Arguments:
- prior_sample_stack: float32 [128, 3, 256, 512], P('mem', None, None, 'slab'), may hold values from -4 to 4
- obs_cell: int32 [128, 512], P('mem', 'slab'), may hold values from 0 to 255
- obs_value: float32 [128, 512], P('mem', 'slab'), may hold values from -4 to 4
- obs_bin: int32 [128, 512], P('mem', 'slab'), may hold values from 0 to 3
Outputs:
- analysis: float32 [128, 3, 256, 512], P('mem', None, None, 'slab')
Inputs may be any that keep to these rules, and one draw needn't show every extreme that they name: obs_cell is local row times 128 plus local column within the observation's region rows and its index of slab's columns.
All inputs are finite; a program needn't handle non-finite values.
Results may differ from a plain program's by a relative error of at most 0.0003.
Values sent between devices are 32-bit elements; how exact they have to be, the bound alone decides.
A program may use at most 64 MiB of HBM per device.

v0:
```python
import math
import jax
import jax.numpy as jnp
from jax import lax
from jax.sharding import PartitionSpec as P

STEPS = 12
SWEEPS = 8
time_step = 0.25
gravity = 1.0
mean_depth = 1.0
coriolis = 0.2
viscosity = 0.4
inflation = 1.1
highest = lax.Precision.HIGHEST


def padded_2(cells, sides, width):
    for axis, dim in sides:
        count = lax.axis_size(axis)
        head = lax.slice_in_dim(cells, 0, width, axis=dim)
        tail = lax.slice_in_dim(cells, cells.shape[dim] - width, cells.shape[dim], axis=dim)
        cells = jnp.concatenate(
            [
                lax.ppermute(tail, axis, [(i, (i + 1) % count) for i in range(count)]),
                cells,
                lax.ppermute(head, axis, [((i + 1) % count, i) for i in range(count)]),
            ],
            axis=dim,
        )
    return cells


def passed_along(value, axis, steps):
    count = lax.axis_size(axis)
    pairs = [(source, (source + steps) % count) for source in range(count)]
    return lax.ppermute(value, axis, pairs)


def sent_to_all(value, axis):
    size = lax.axis_size(axis)
    return lax.all_to_all(
        jnp.broadcast_to(value[None], (size, *value.shape)), axis, 0, 0, tiled=True
    )


def over_copies(value, axis):
    return sent_to_all(value, axis).sum(axis=0)


def together(arrays, axis):
    ends = [0]
    for a in arrays:
        ends.append(ends[-1] + a.size)
    running = over_copies(jnp.concatenate([a.ravel() for a in arrays]), axis)
    return tuple((running[b:e].reshape(a.shape) for a, b, e in zip(arrays, ends, ends[1:])))


def centre(values):
    return values[:, 1:-1]


def east_of(values):
    return jnp.roll(values[:, 1:-1], -1, 0)


def west_of(values):
    return jnp.roll(values[:, 1:-1], 1, 0)


def north_of(values):
    return values[:, 2:]


def south_of(values):
    return values[:, :-2]


def spread(values):
    return (
        east_of(values)
        + west_of(values)
        + north_of(values)
        + south_of(values)
        - 4.0 * centre(values)
    )


def slope_x(values):
    return 0.5 * (east_of(values) - west_of(values))


def slope_y(values):
    return 0.5 * (north_of(values) - south_of(values))


def advance(padded):
    elevation_anomaly = padded[0]
    east_wind = padded[1]
    north_wind = padded[2]
    flux_x = (mean_depth + elevation_anomaly) * east_wind
    flux_y = (mean_depth + elevation_anomaly) * north_wind
    east_mid = centre(east_wind)
    north_mid = centre(north_wind)
    new_height = centre(elevation_anomaly) + time_step * (
        viscosity * spread(elevation_anomaly) - slope_x(flux_x) - slope_y(flux_y)
    )
    new_east = east_mid + time_step * (
        viscosity * spread(east_wind)
        - east_mid * slope_x(east_wind)
        - north_mid * slope_y(east_wind)
        - gravity * slope_x(elevation_anomaly)
        + coriolis * north_mid
    )
    new_north = north_mid + time_step * (
        viscosity * spread(north_wind)
        - east_mid * slope_x(north_wind)
        - north_mid * slope_y(north_wind)
        - gravity * slope_y(elevation_anomaly)
        - coriolis * east_mid
    )
    return jnp.stack([new_height, new_east, new_north])


def partial_sums(anomaly, distance, obs_weight, innovation, band_rows):
    target = jnp.arange(band_rows).astype(jnp.float32)
    scaled_dist = (distance[None, :] - target[:, None]) / float(band_rows)
    weight = obs_weight[None, :] * jnp.exp(-0.5 * scaled_dist * scaled_dist)
    scaled = anomaly[None, :, :] * weight[:, None, :]
    gram_matrix = jnp.einsum("tmj,kj->tmk", scaled, anomaly, precision=highest)
    pull_vector = jnp.einsum("tmj,j->tm", scaled, innovation, precision=highest)
    return (gram_matrix, pull_vector)


def batch_product(left, right):
    return jnp.einsum("tij,tjk->tik", left, right, precision=highest)


def weights_from(gram_matrix, pull_vector, members):
    identity = jnp.eye(members, dtype=jnp.float32)
    gram_matrix = gram_matrix + (members - 1) / inflation * identity[None]
    traces = jnp.trace(gram_matrix, axis1=1, axis2=2)
    iterate = gram_matrix / traces[:, None, None]
    inverse = jnp.broadcast_to(identity, gram_matrix.shape)
    for iteration in range(SWEEPS):
        correction = 1.5 * identity[None] - 0.5 * batch_product(inverse, iterate)
        iterate, inverse = (batch_product(iterate, correction), batch_product(correction, inverse))
    inv_root = inverse / jnp.sqrt(traces)[:, None, None]
    inner = jnp.einsum("tij,tj->ti", inv_root, pull_vector, precision=highest)
    mean_weights = jnp.einsum("tij,tj->ti", inv_root, inner, precision=highest)
    return math.sqrt(members - 1) * inv_root + mean_weights[:, :, None]


def apply_weights(zone_portion, mixing):
    mean_state = jnp.mean(zone_portion, axis=0)
    spread_state = zone_portion - mean_state[None]
    return mean_state[None] + jnp.einsum("mftc,tmk->kftc", spread_state, mixing, precision=highest)


def local(prior_sample_stack, obs_cell, obs_value, obs_bin):
    current_condition = prior_sample_stack[0]

    def four_steps(counter, values):
        padded = padded_2(values, (("slab", 2),), 4)
        for substep in range(4):
            padded = advance(padded)
        return padded

    current_condition = lax.fori_loop(0, STEPS // 4, four_steps, current_condition)
    predicted_grid = current_condition[None]
    zone_collection = lax.all_to_all(predicted_grid, "mem", split_axis=2, concat_axis=0, tiled=True)
    heights = zone_collection[:, 0]
    members = heights.shape[0]
    band_rows = heights.shape[1]
    columns = heights.shape[2]
    observed = jnp.take(heights.reshape(members, band_rows * columns), obs_cell[0], axis=1)
    obs_mean = jnp.mean(observed, axis=0)
    anomaly = observed - obs_mean[None]
    extras = jnp.stack(
        [
            obs_value[0] - obs_mean,
            10.0 / (1.0 + obs_bin[0].astype(jnp.float32)),
            (obs_cell[0] // columns).astype(jnp.float32),
        ]
    )
    package = (anomaly, extras)
    collected = [(0, package)]
    for stride in (1, -1, 2, -2):
        collected.append((-stride, passed_along((package[0], package[1]), "mem", stride)))
    all_anomaly = jnp.concatenate([entry[1][0] for entry in collected], axis=1)
    distance = jnp.concatenate(
        [entry[1][1][2] + float(entry[0] * band_rows) for entry in collected]
    )
    obs_weight = jnp.concatenate([entry[1][1][1] for entry in collected])
    innovation = jnp.concatenate([entry[1][1][0] for entry in collected])
    gram_matrix, pull_vector = partial_sums(
        all_anomaly, distance, obs_weight, innovation, band_rows
    )
    gram_matrix, pull_vector = together((gram_matrix, pull_vector), "slab")
    mixing = weights_from(gram_matrix, pull_vector, members)
    return lax.all_to_all(
        apply_weights(zone_collection, mixing), "mem", split_axis=0, concat_axis=2, tiled=True
    )


def solution(mesh):
    placed = (P("mem", None, None, "slab"), P("mem", "slab"), P("mem", "slab"), P("mem", "slab"))
    return jax.shard_map(
        local, mesh=mesh, in_specs=placed, out_specs=P("mem", None, None, "slab"), check_vma=False
    )
```

profile of v0, /device:TPU:1, one launch (start us, length us, event | category | flops | bytes accessed | tf_op | source)
XLA Modules:
  0.0 343.0 jit_solution(7744454603862353869)
XLA Ops:
  0.0 1.0 copy-done
  1.0 111.7 %while.10 = (s32[]{:T(128)}, f32[3,256,128]{2,1,0:T(8,128)S(1)}, s32[]{:T(128)}) while((s32[]{:T(128)}, f32[3,256,128]{2,1,0:T(8,128)S(1)}, s32[]{:T(128)}) %tuple.159), condition=%wide.region_1.2_spmd, body=%wide.region_0.1_spmd.sunk | while | flops 9566210 | bytes 27316348 | solution.py:169
  1.2 8.7 %collective-permute-start = (f32[3,256,4]{2,1,0:T(8,128)S(1)}, f32[3,256,4]{2,1,0:T(8,128)S(1)}, u32[]{:S(2)}, u32[]{:S(2)}) collective-permute-start(f32[3,256,4]{2,1,0:T(8,128)S(1)} %get-tuple-element.233), channel_id=1, source_target_pairs={{1,0},{2,1},{3,2},{0,3},{5,4},{6,5},{7,6},{4,7},{9,8},{10,9},{11,1... | collective-permute-start | bytes 36872 | tf_op jit(solution)/shard_map/while/body/eval_jaxpr/ppermute | solution.py:27
  9.9 10.0 %collective-permute-start.1 = (f32[3,256,4]{2,1,0:T(8,128)S(1)}, f32[3,256,4]{2,1,0:T(8,128)S(1)}, u32[]{:S(2)}, u32[]{:S(2)}) collective-permute-start(f32[3,256,4]{2,1,0:T(8,128)S(1)} %get-tuple-element.234), channel_id=1, source_target_pairs={{0,1},{1,2},{2,3},{3,0},{4,5},{5,6},{6,7},{7,4},{8,9},{9,10},{10,1... | collective-permute-start | bytes 36872 | tf_op jit(solution)/shard_map/while/body/eval_jaxpr/ppermute | solution.py:25
  19.9 3.8 %collective-permute-done = f32[3,256,4]{2,1,0:T(8,128)S(1)} collective-permute-done((f32[3,256,4]{2,1,0:T(8,128)S(1)}, f32[3,256,4]{2,1,0:T(8,128)S(1)}, u32[]{:S(2)}, u32[]{:S(2)}) %collective-permute-start) | collective-permute-done | bytes 12320 | tf_op jit(solution)/shard_map/while/body/eval_jaxpr/ppermute | solution.py:27
  23.7 18.3 %collective-permute-done.1 = f32[3,256,4]{2,1,0:T(8,128)S(1)} collective-permute-done((f32[3,256,4]{2,1,0:T(8,128)S(1)}, f32[3,256,4]{2,1,0:T(8,128)S(1)}, u32[]{:S(2)}, u32[]{:S(2)}) %collective-permute-start.1) | collective-permute-done | bytes 12320 | tf_op jit(solution)/shard_map/while/body/eval_jaxpr/ppermute | solution.py:25
  43.4 0.6 add_multiply_fusion.16
  45.4 0.6 add_multiply_fusion.18
  47.5 0.6 add_multiply_fusion.20
  50.1 3.3 collective-permute-start
  53.4 11.9 %collective-permute-start.1 = (f32[3,256,4]{2,1,0:T(8,128)S(1)}, f32[3,256,4]{2,1,0:T(8,128)S(1)}, u32[]{:S(2)}, u32[]{:S(2)}) collective-permute-start(f32[3,256,4]{2,1,0:T(8,128)S(1)} %get-tuple-element.234), channel_id=1, source_target_pairs={{0,1},{1,2},{2,3},{3,0},{4,5},{5,6},{6,7},{7,4},{8,9},{9,10},{10,1... | collective-permute-start | bytes 36872 | tf_op jit(solution)/shard_map/while/body/eval_jaxpr/ppermute | solution.py:25
  65.4 11.8 %collective-permute-done = f32[3,256,4]{2,1,0:T(8,128)S(1)} collective-permute-done((f32[3,256,4]{2,1,0:T(8,128)S(1)}, f32[3,256,4]{2,1,0:T(8,128)S(1)}, u32[]{:S(2)}, u32[]{:S(2)}) %collective-permute-start) | collective-permute-done | bytes 12320 | tf_op jit(solution)/shard_map/while/body/eval_jaxpr/ppermute | solution.py:27
  77.1 0.4 pad_maximum_fusion.30
  78.5 0.6 add_multiply_fusion.16
  80.5 0.6 add_multiply_fusion.18
  82.6 0.6 add_multiply_fusion.20
  85.2 5.1 %collective-permute-start = (f32[3,256,4]{2,1,0:T(8,128)S(1)}, f32[3,256,4]{2,1,0:T(8,128)S(1)}, u32[]{:S(2)}, u32[]{:S(2)}) collective-permute-start(f32[3,256,4]{2,1,0:T(8,128)S(1)} %get-tuple-element.233), channel_id=1, source_target_pairs={{1,0},{2,1},{3,2},{0,3},{5,4},{6,5},{7,6},{4,7},{9,8},{10,9},{11,1... | collective-permute-start | bytes 36872 | tf_op jit(solution)/shard_map/while/body/eval_jaxpr/ppermute | solution.py:27
  90.3 9.4 %collective-permute-start.1 = (f32[3,256,4]{2,1,0:T(8,128)S(1)}, f32[3,256,4]{2,1,0:T(8,128)S(1)}, u32[]{:S(2)}, u32[]{:S(2)}) collective-permute-start(f32[3,256,4]{2,1,0:T(8,128)S(1)} %get-tuple-element.234), channel_id=1, source_target_pairs={{0,1},{1,2},{2,3},{3,0},{4,5},{5,6},{6,7},{7,4},{8,9},{9,10},{10,1... | collective-permute-start | bytes 36872 | tf_op jit(solution)/shard_map/while/body/eval_jaxpr/ppermute | solution.py:25
  99.7 5.1 %collective-permute-done = f32[3,256,4]{2,1,0:T(8,128)S(1)} collective-permute-done((f32[3,256,4]{2,1,0:T(8,128)S(1)}, f32[3,256,4]{2,1,0:T(8,128)S(1)}, u32[]{:S(2)}, u32[]{:S(2)}) %collective-permute-start) | collective-permute-done | bytes 12320 | tf_op jit(solution)/shard_map/while/body/eval_jaxpr/ppermute | solution.py:27
  106.2 0.6 add_multiply_fusion.16
  108.2 0.6 add_multiply_fusion.18
  110.3 0.6 add_multiply_fusion.20
  112.7 1.2 copy.44
  113.9 47.4 %all-to-all-start = ((f32[1,3,256,128]{3,0,1,2:T(1,128)}), f32[1,3,256,128]{3,0,1,2:T(1,128)S(1)}, u32[]{:S(2)}, u32[]{:S(2)}) async-start(f32[1,3,256,128]{3,0,1,2:T(1,128)} %copy.44), calls=%async_computation | async-start | bytes 786432 | tf_op jit(solution)/shard_map/all_to_all | solution.py:171
  161.3 0.6 copy-done.3
  162.0 0.6 copy-done.4
  162.6 23.9 %all-to-all-done = f32[1,3,256,128]{3,0,1,2:T(1,128)S(1)} async-done(((f32[1,3,256,128]{3,0,1,2:T(1,128)}), f32[1,3,256,128]{3,0,1,2:T(1,128)S(1)}, u32[]{:S(2)}, u32[]{:S(2)}) %all-to-all-start) | async-done | bytes 393248 | tf_op jit(solution)/shard_map/all_to_all | solution.py:171
  186.7 0.6 gather_fusion
  187.5 0.6 copy-done.2
  188.2 2.6 collective-permute-start.6
  190.8 13.5 %collective-permute-start.7 = (f32[3,128]{1,0:T(4,128)S(1)}, f32[3,128]{1,0:T(4,128)S(1)}, u32[]{:S(2)}, u32[]{:S(2)}) collective-permute-start(f32[3,128]{1,0:T(4,128)S(1)} %pad_maximum_fusion.27), channel_id=1, source_target_pairs={{0,508},{4,0},{8,4},{12,8},{16,12},{20,16},{24,20},{28,24},{32,28}... | collective-permute-start | bytes 4616 | tf_op jit(solution)/shard_map/ppermute | solution.py:37
  204.3 1.9 collective-permute-start.8
  206.2 13.3 %collective-permute-start.9 = (f32[3,128]{1,0:T(4,128)S(1)}, f32[3,128]{1,0:T(4,128)S(1)}, u32[]{:S(2)}, u32[]{:S(2)}) collective-permute-start(f32[3,128]{1,0:T(4,128)S(1)} %pad_maximum_fusion.27), channel_id=1, source_target_pairs={{0,504},{4,508},{8,0},{12,4},{16,8},{20,12},{24,16},{28,20},{32,24... | collective-permute-start | bytes 4616 | tf_op jit(solution)/shard_map/ppermute | solution.py:37
  219.5 1.9 collective-permute-start.2
  221.5 14.2 %collective-permute-start.3 = (f32[128,128]{1,0:T(8,128)S(1)}, f32[128,128]{1,0:T(8,128)S(1)}, u32[]{:S(2)}, u32[]{:S(2)}) collective-permute-start(f32[128,128]{1,0:T(8,128)S(1)} %get-tuple-element.38), channel_id=1, source_target_pairs={{0,508},{4,0},{8,4},{12,8},{16,12},{20,16},{24,20},{28,24},{32,28}... | collective-permute-start | bytes 196616 | tf_op jit(solution)/shard_map/ppermute | solution.py:37
  235.7 1.9 collective-permute-start.4
  237.7 13.3 %collective-permute-start.5 = (f32[128,128]{1,0:T(8,128)S(1)}, f32[128,128]{1,0:T(8,128)S(1)}, u32[]{:S(2)}, u32[]{:S(2)}) collective-permute-start(f32[128,128]{1,0:T(8,128)S(1)} %get-tuple-element.38), channel_id=1, source_target_pairs={{0,504},{4,508},{8,0},{12,4},{16,8},{20,12},{24,16},{28,20},{32,24... | collective-permute-start | bytes 196616 | tf_op jit(solution)/shard_map/ppermute | solution.py:37
  251.2 1.1 collective-permute-done.5
  252.3 0.7 fusion.36
  253.0 0.6 fusion.34
  253.7 1.1 broadcast_in_dim.31
  254.8 20.6 %all-to-all-start.1 = ((f32[4,1,33024]{2,1,0:T(1,128)}), f32[4,1,33024]{2,1,0:T(1,128)S(1)}, u32[]{:S(2)}, u32[]{:S(2)}) async-start(f32[4,1,33024]{2,1,0:T(1,128)} %broadcast_in_dim.31), calls=%async_computation.1 | async-start | bytes 1056768 | tf_op jit(solution)/shard_map/all_to_all | solution.py:42
  275.4 16.5 %all-to-all-done.1 = f32[4,1,33024]{2,1,0:T(1,128)S(1)} async-done(((f32[4,1,33024]{2,1,0:T(1,128)}), f32[4,1,33024]{2,1,0:T(1,128)S(1)}, u32[]{:S(2)}, u32[]{:S(2)}) %all-to-all-start.1) | async-done | bytes 528416 | tf_op jit(solution)/shard_map/all_to_all | solution.py:42
  291.9 0.5 reduce_sum.39
  299.1 0.7 slice-done
  300.4 0.6 fusion.25
  301.3 40.8 %all_to_all.42 = f32[128,3,2,128]{3,2,1,0:T(2,128)S(1)} all-to-all(f32[128,3,2,128]{3,2,1,0:T(2,128)S(1)} %copy.51), channel_id=1, replica_groups=mesh['mem'=128,'slab'=4] {'mem'}, dimensions={0} | all-to-all | bytes 786432 | tf_op jit(solution)/shard_map/all_to_all | solution.py:201
  342.1 0.9 copy.52
  (198 shorter events, 26.2 us)
Async XLA Ops:
  0.0 1.0 copy-start
  1.2 22.6 %collective-permute-start = (f32[3,256,4]{2,1,0:T(8,128)S(1)}, f32[3,256,4]{2,1,0:T(8,128)S(1)}, u32[]{:S(2)}, u32[]{:S(2)}) collective-permute-start(f32[3,256,4]{2,1,0:T(8,128)S(1)} %get-tuple-element.233), channel_id=1, source_target_pairs={{1,0},{2,1},{3,2},{0,3},{5,4},{6,5},{7,6},{4,7},{9,8},{10,9},{11,1... | collective-permute-start | bytes 36872 | tf_op jit(solution)/shard_map/while/body/eval_jaxpr/ppermute | solution.py:27
  9.9 32.1 %collective-permute-start.1 = (f32[3,256,4]{2,1,0:T(8,128)S(1)}, f32[3,256,4]{2,1,0:T(8,128)S(1)}, u32[]{:S(2)}, u32[]{:S(2)}) collective-permute-start(f32[3,256,4]{2,1,0:T(8,128)S(1)} %get-tuple-element.234), channel_id=1, source_target_pairs={{0,1},{1,2},{2,3},{3,0},{4,5},{5,6},{6,7},{7,4},{8,9},{9,10},{10,1... | collective-permute-start | bytes 36872 | tf_op jit(solution)/shard_map/while/body/eval_jaxpr/ppermute | solution.py:25
  50.1 27.0 %collective-permute-start = (f32[3,256,4]{2,1,0:T(8,128)S(1)}, f32[3,256,4]{2,1,0:T(8,128)S(1)}, u32[]{:S(2)}, u32[]{:S(2)}) collective-permute-start(f32[3,256,4]{2,1,0:T(8,128)S(1)} %get-tuple-element.233), channel_id=1, source_target_pairs={{1,0},{2,1},{3,2},{0,3},{5,4},{6,5},{7,6},{4,7},{9,8},{10,9},{11,1... | collective-permute-start | bytes 36872 | tf_op jit(solution)/shard_map/while/body/eval_jaxpr/ppermute | solution.py:27
  53.4 23.7 %collective-permute-start.1 = (f32[3,256,4]{2,1,0:T(8,128)S(1)}, f32[3,256,4]{2,1,0:T(8,128)S(1)}, u32[]{:S(2)}, u32[]{:S(2)}) collective-permute-start(f32[3,256,4]{2,1,0:T(8,128)S(1)} %get-tuple-element.234), channel_id=1, source_target_pairs={{0,1},{1,2},{2,3},{3,0},{4,5},{5,6},{6,7},{7,4},{8,9},{9,10},{10,1... | collective-permute-start | bytes 36872 | tf_op jit(solution)/shard_map/while/body/eval_jaxpr/ppermute | solution.py:25
  85.2 19.6 %collective-permute-start = (f32[3,256,4]{2,1,0:T(8,128)S(1)}, f32[3,256,4]{2,1,0:T(8,128)S(1)}, u32[]{:S(2)}, u32[]{:S(2)}) collective-permute-start(f32[3,256,4]{2,1,0:T(8,128)S(1)} %get-tuple-element.233), channel_id=1, source_target_pairs={{1,0},{2,1},{3,2},{0,3},{5,4},{6,5},{7,6},{4,7},{9,8},{10,9},{11,1... | collective-permute-start | bytes 36872 | tf_op jit(solution)/shard_map/while/body/eval_jaxpr/ppermute | solution.py:27
  90.3 14.5 %collective-permute-start.1 = (f32[3,256,4]{2,1,0:T(8,128)S(1)}, f32[3,256,4]{2,1,0:T(8,128)S(1)}, u32[]{:S(2)}, u32[]{:S(2)}) collective-permute-start(f32[3,256,4]{2,1,0:T(8,128)S(1)} %get-tuple-element.234), channel_id=1, source_target_pairs={{0,1},{1,2},{2,3},{3,0},{4,5},{5,6},{6,7},{7,4},{8,9},{9,10},{10,1... | collective-permute-start | bytes 36872 | tf_op jit(solution)/shard_map/while/body/eval_jaxpr/ppermute | solution.py:25
  113.9 72.7 %all-to-all-start = ((f32[1,3,256,128]{3,0,1,2:T(1,128)}), f32[1,3,256,128]{3,0,1,2:T(1,128)S(1)}, u32[]{:S(2)}, u32[]{:S(2)}) async-start(f32[1,3,256,128]{3,0,1,2:T(1,128)} %copy.44), calls=%async_computation | async-start | bytes 786432 | tf_op jit(solution)/shard_map/all_to_all | solution.py:171
  161.3 0.7 copy-start.3
  162.0 0.7 copy-start.4
  187.5 0.7 copy-start.2
  188.2 33.3 %collective-permute-start.6 = (f32[3,128]{1,0:T(4,128)S(1)}, f32[3,128]{1,0:T(4,128)S(1)}, u32[]{:S(2)}, u32[]{:S(2)}) collective-permute-start(f32[3,128]{1,0:T(4,128)S(1)} %pad_maximum_fusion.27), channel_id=1, source_target_pairs={{0,4},{4,8},{8,12},{12,16},{16,20},{20,24},{24,28},{28,32},{32,36}... | collective-permute-start | bytes 4616 | tf_op jit(solution)/shard_map/ppermute | solution.py:37
  190.8 44.9 %collective-permute-start.7 = (f32[3,128]{1,0:T(4,128)S(1)}, f32[3,128]{1,0:T(4,128)S(1)}, u32[]{:S(2)}, u32[]{:S(2)}) collective-permute-start(f32[3,128]{1,0:T(4,128)S(1)} %pad_maximum_fusion.27), channel_id=1, source_target_pairs={{0,508},{4,0},{8,4},{12,8},{16,12},{20,16},{24,20},{28,24},{32,28}... | collective-permute-start | bytes 4616 | tf_op jit(solution)/shard_map/ppermute | solution.py:37
  204.3 33.4 %collective-permute-start.8 = (f32[3,128]{1,0:T(4,128)S(1)}, f32[3,128]{1,0:T(4,128)S(1)}, u32[]{:S(2)}, u32[]{:S(2)}) collective-permute-start(f32[3,128]{1,0:T(4,128)S(1)} %pad_maximum_fusion.27), channel_id=1, source_target_pairs={{0,8},{4,12},{8,16},{12,20},{16,24},{20,28},{24,32},{28,36},{32,40... | collective-permute-start | bytes 4616 | tf_op jit(solution)/shard_map/ppermute | solution.py:37
  206.2 44.8 %collective-permute-start.9 = (f32[3,128]{1,0:T(4,128)S(1)}, f32[3,128]{1,0:T(4,128)S(1)}, u32[]{:S(2)}, u32[]{:S(2)}) collective-permute-start(f32[3,128]{1,0:T(4,128)S(1)} %pad_maximum_fusion.27), channel_id=1, source_target_pairs={{0,504},{4,508},{8,0},{12,4},{16,8},{20,12},{24,16},{28,20},{32,24... | collective-permute-start | bytes 4616 | tf_op jit(solution)/shard_map/ppermute | solution.py:37
  219.5 31.6 %collective-permute-start.2 = (f32[128,128]{1,0:T(8,128)S(1)}, f32[128,128]{1,0:T(8,128)S(1)}, u32[]{:S(2)}, u32[]{:S(2)}) collective-permute-start(f32[128,128]{1,0:T(8,128)S(1)} %get-tuple-element.38), channel_id=1, source_target_pairs={{0,4},{4,8},{8,12},{12,16},{16,20},{20,24},{24,28},{28,32},{32,36}... | collective-permute-start | bytes 196616 | tf_op jit(solution)/shard_map/ppermute | solution.py:37
  221.5 29.6 %collective-permute-start.3 = (f32[128,128]{1,0:T(8,128)S(1)}, f32[128,128]{1,0:T(8,128)S(1)}, u32[]{:S(2)}, u32[]{:S(2)}) collective-permute-start(f32[128,128]{1,0:T(8,128)S(1)} %get-tuple-element.38), channel_id=1, source_target_pairs={{0,508},{4,0},{8,4},{12,8},{16,12},{20,16},{24,20},{28,24},{32,28}... | collective-permute-start | bytes 196616 | tf_op jit(solution)/shard_map/ppermute | solution.py:37
  235.7 15.5 %collective-permute-start.4 = (f32[128,128]{1,0:T(8,128)S(1)}, f32[128,128]{1,0:T(8,128)S(1)}, u32[]{:S(2)}, u32[]{:S(2)}) collective-permute-start(f32[128,128]{1,0:T(8,128)S(1)} %get-tuple-element.38), channel_id=1, source_target_pairs={{0,8},{4,12},{8,16},{12,20},{16,24},{20,28},{24,32},{28,36},{32,40... | collective-permute-start | bytes 196616 | tf_op jit(solution)/shard_map/ppermute | solution.py:37
  237.7 14.6 %collective-permute-start.5 = (f32[128,128]{1,0:T(8,128)S(1)}, f32[128,128]{1,0:T(8,128)S(1)}, u32[]{:S(2)}, u32[]{:S(2)}) collective-permute-start(f32[128,128]{1,0:T(8,128)S(1)} %get-tuple-element.38), channel_id=1, source_target_pairs={{0,504},{4,508},{8,0},{12,4},{16,8},{20,12},{24,16},{28,20},{32,24... | collective-permute-start | bytes 196616 | tf_op jit(solution)/shard_map/ppermute | solution.py:37
  254.8 37.2 %all-to-all-start.1 = ((f32[4,1,33024]{2,1,0:T(1,128)}), f32[4,1,33024]{2,1,0:T(1,128)S(1)}, u32[]{:S(2)}, u32[]{:S(2)}) async-start(f32[4,1,33024]{2,1,0:T(1,128)} %broadcast_in_dim.31), calls=%async_computation.1 | async-start | bytes 1056768 | tf_op jit(solution)/shard_map/all_to_all | solution.py:42
  292.4 6.1 %copy-start.1 = (f32[33024]{0:T(1024)}, f32[33024]{0:T(1024)S(1)}, u32[]{:S(2)}) copy-start(f32[33024]{0:T(1024)S(1)} %reduce_sum.39) | copy-start | bytes 396292
  299.1 0.7 slice-start
where the time goes:
time: 344 us; the launch traced here: 343 us
  starting transfers between devices  179 us (52%)
  waiting for transfers between devices  80.5 us (23%)
  blocking collectives  40.8 us (12%)
  local copies, waits for them, and re-layouts  20.2 us (6%)
  other arithmetic  12.4 us (4%)
  matrix products  8.87 us (3%)
    ppermute x8, starting transfers between devices, passed_along(): return lax.ppermute(value, axis, pairs)  62.6 us
    all_to_all x1, starting transfers between devices, local(): lax.all_to_all(predicted_grid, 'mem', split_axis=2, concat_axis=0, tiled=...  47.4 us
    all_to_all x1, blocking collectives, local(): lax.all_to_all(apply_weights(zone_collection, mixing), 'mem', split_axis=...  40.8 us
    ppermute x3, starting transfers between devices, padded_2(): lax.ppermute(tail, axis, [(i, (i + 1) % count) for i in range(count)])  31.3 us
    all_to_all x1, waiting for transfers between devices, local(): lax.all_to_all(predicted_grid, 'mem', split_axis=2, concat_axis=0, tiled=...  23.9 us
    ppermute x3, waiting for transfers between devices, padded_2(): lax.ppermute(head, axis, [((i + 1) % count, i) for i in range(count)])  20.7 us
    all_to_all x1, starting transfers between devices, sent_to_all(): lax.all_to_all(jnp.broadcast_to(value[None], (size, *value.shape)), axis,...  20.6 us
    ppermute x3, waiting for transfers between devices, padded_2(): lax.ppermute(tail, axis, [(i, (i + 1) % count) for i in range(count)])  18.3 us
  transfers between devices with their start and end apart: 16, of which 7 were waited for; matrix products, arithmetic and copies ran while one was open for 0% of the time, Pallas kernels for 0%

commit v1 on v0

--- a/solution.py
+++ b/solution.py
@@ -198,8 +198,16 @@
     )
     gram_matrix, pull_vector = together((gram_matrix, pull_vector), "slab")
     mixing = weights_from(gram_matrix, pull_vector, members)
-    return lax.all_to_all(
-        apply_weights(zone_collection, mixing), "mem", split_axis=0, concat_axis=2, tiled=True
+    return jnp.concatenate(
+        lax.all_to_all(
+            jnp.stack(
+                jnp.split(apply_weights(zone_collection, mixing), lax.axis_size("mem"), axis=0)
+            ),
+            "mem",
+            0,
+            0,
+        ),
+        axis=2,
     )
 
 

time: 344 us -> 346 us (level)
  no operation moved by 1% of the time
where the time goes in v1:
time: 346 us; the launch traced here: 345 us
  starting transfers between devices  179 us (52%)
  waiting for transfers between devices  80.3 us (23%)
  blocking collectives  40.8 us (12%)
  local copies, waits for them, and re-layouts  21.6 us (6%)
  other arithmetic  12.5 us (4%)
  matrix products  8.87 us (3%)
    ppermute x8, starting transfers between devices, passed_along(): return lax.ppermute(value, axis, pairs)  62.6 us
    all_to_all x1, starting transfers between devices, local(): lax.all_to_all(predicted_grid, 'mem', split_axis=2, concat_axis=0, tiled=...  47.4 us
    all_to_all x1, blocking collectives, local(): lax.all_to_all(jnp.stack(jnp.split(apply_weights(zone_collection, mixing)...  40.8 us
    ppermute x3, starting transfers between devices, padded_2(): lax.ppermute(tail, axis, [(i, (i + 1) % count) for i in range(count)])  31.3 us
    all_to_all x1, waiting for transfers between devices, local(): lax.all_to_all(predicted_grid, 'mem', split_axis=2, concat_axis=0, tiled=...  23.9 us
    ppermute x3, waiting for transfers between devices, padded_2(): lax.ppermute(head, axis, [((i + 1) % count, i) for i in range(count)])  20.7 us
    all_to_all x1, starting transfers between devices, sent_to_all(): lax.all_to_all(jnp.broadcast_to(value[None], (size, *value.shape)), axis,...  20.6 us
    ppermute x3, waiting for transfers between devices, padded_2(): lax.ppermute(tail, axis, [(i, (i + 1) % count) for i in range(count)])  18.3 us
  transfers between devices with their start and end apart: 16, of which 7 were waited for; matrix products, arithmetic and copies ran while one was open for 0% of the time, Pallas kernels for 0%

profile of v1, /device:TPU:1, one launch (start us, length us, event | category | flops | bytes accessed | tf_op | source)
XLA Modules:
  0.0 345.1 jit_solution(12778864894171161533)
XLA Ops:
  0.0 1.0 copy-done
  1.0 111.7 %while.10 = (s32[]{:T(128)}, f32[3,256,128]{2,1,0:T(8,128)S(1)}, s32[]{:T(128)}) while((s32[]{:T(128)}, f32[3,256,128]{2,1,0:T(8,128)S(1)}, s32[]{:T(128)}) %tuple.295), condition=%wide.region_1.2_spmd, body=%wide.region_0.1_spmd.sunk | while | flops 9566210 | bytes 27316348 | solution.py:169
  1.2 8.7 %collective-permute-start = (f32[3,256,4]{2,1,0:T(8,128)S(1)}, f32[3,256,4]{2,1,0:T(8,128)S(1)}, u32[]{:S(2)}, u32[]{:S(2)}) collective-permute-start(f32[3,256,4]{2,1,0:T(8,128)S(1)} %get-tuple-element.391), channel_id=1, source_target_pairs={{1,0},{2,1},{3,2},{0,3},{5,4},{6,5},{7,6},{4,7},{9,8},{10,9},{11,1... | collective-permute-start | bytes 36872 | tf_op jit(solution)/shard_map/while/body/eval_jaxpr/ppermute | solution.py:27
  9.9 10.0 %collective-permute-start.1 = (f32[3,256,4]{2,1,0:T(8,128)S(1)}, f32[3,256,4]{2,1,0:T(8,128)S(1)}, u32[]{:S(2)}, u32[]{:S(2)}) collective-permute-start(f32[3,256,4]{2,1,0:T(8,128)S(1)} %get-tuple-element.392), channel_id=1, source_target_pairs={{0,1},{1,2},{2,3},{3,0},{4,5},{5,6},{6,7},{7,4},{8,9},{9,10},{10,1... | collective-permute-start | bytes 36872 | tf_op jit(solution)/shard_map/while/body/eval_jaxpr/ppermute | solution.py:25
  19.9 3.8 %collective-permute-done = f32[3,256,4]{2,1,0:T(8,128)S(1)} collective-permute-done((f32[3,256,4]{2,1,0:T(8,128)S(1)}, f32[3,256,4]{2,1,0:T(8,128)S(1)}, u32[]{:S(2)}, u32[]{:S(2)}) %collective-permute-start) | collective-permute-done | bytes 12320 | tf_op jit(solution)/shard_map/while/body/eval_jaxpr/ppermute | solution.py:27
  23.7 18.3 %collective-permute-done.1 = f32[3,256,4]{2,1,0:T(8,128)S(1)} collective-permute-done((f32[3,256,4]{2,1,0:T(8,128)S(1)}, f32[3,256,4]{2,1,0:T(8,128)S(1)}, u32[]{:S(2)}, u32[]{:S(2)}) %collective-permute-start.1) | collective-permute-done | bytes 12320 | tf_op jit(solution)/shard_map/while/body/eval_jaxpr/ppermute | solution.py:25
  43.4 0.6 add_multiply_fusion.16
  45.4 0.6 add_multiply_fusion.18
  47.5 0.6 add_multiply_fusion.20
  50.1 3.3 collective-permute-start
  53.4 11.9 %collective-permute-start.1 = (f32[3,256,4]{2,1,0:T(8,128)S(1)}, f32[3,256,4]{2,1,0:T(8,128)S(1)}, u32[]{:S(2)}, u32[]{:S(2)}) collective-permute-start(f32[3,256,4]{2,1,0:T(8,128)S(1)} %get-tuple-element.392), channel_id=1, source_target_pairs={{0,1},{1,2},{2,3},{3,0},{4,5},{5,6},{6,7},{7,4},{8,9},{9,10},{10,1... | collective-permute-start | bytes 36872 | tf_op jit(solution)/shard_map/while/body/eval_jaxpr/ppermute | solution.py:25
  65.4 11.8 %collective-permute-done = f32[3,256,4]{2,1,0:T(8,128)S(1)} collective-permute-done((f32[3,256,4]{2,1,0:T(8,128)S(1)}, f32[3,256,4]{2,1,0:T(8,128)S(1)}, u32[]{:S(2)}, u32[]{:S(2)}) %collective-permute-start) | collective-permute-done | bytes 12320 | tf_op jit(solution)/shard_map/while/body/eval_jaxpr/ppermute | solution.py:27
  77.1 0.4 pad_maximum_fusion.30
  78.5 0.6 add_multiply_fusion.16
  80.5 0.6 add_multiply_fusion.18
  82.6 0.6 add_multiply_fusion.20
  85.2 5.1 %collective-permute-start = (f32[3,256,4]{2,1,0:T(8,128)S(1)}, f32[3,256,4]{2,1,0:T(8,128)S(1)}, u32[]{:S(2)}, u32[]{:S(2)}) collective-permute-start(f32[3,256,4]{2,1,0:T(8,128)S(1)} %get-tuple-element.391), channel_id=1, source_target_pairs={{1,0},{2,1},{3,2},{0,3},{5,4},{6,5},{7,6},{4,7},{9,8},{10,9},{11,1... | collective-permute-start | bytes 36872 | tf_op jit(solution)/shard_map/while/body/eval_jaxpr/ppermute | solution.py:27
  90.3 9.4 %collective-permute-start.1 = (f32[3,256,4]{2,1,0:T(8,128)S(1)}, f32[3,256,4]{2,1,0:T(8,128)S(1)}, u32[]{:S(2)}, u32[]{:S(2)}) collective-permute-start(f32[3,256,4]{2,1,0:T(8,128)S(1)} %get-tuple-element.392), channel_id=1, source_target_pairs={{0,1},{1,2},{2,3},{3,0},{4,5},{5,6},{6,7},{7,4},{8,9},{9,10},{10,1... | collective-permute-start | bytes 36872 | tf_op jit(solution)/shard_map/while/body/eval_jaxpr/ppermute | solution.py:25
  99.7 5.1 %collective-permute-done = f32[3,256,4]{2,1,0:T(8,128)S(1)} collective-permute-done((f32[3,256,4]{2,1,0:T(8,128)S(1)}, f32[3,256,4]{2,1,0:T(8,128)S(1)}, u32[]{:S(2)}, u32[]{:S(2)}) %collective-permute-start) | collective-permute-done | bytes 12320 | tf_op jit(solution)/shard_map/while/body/eval_jaxpr/ppermute | solution.py:27
  106.2 0.6 add_multiply_fusion.16
  108.2 0.6 add_multiply_fusion.18
  110.3 0.6 add_multiply_fusion.20
  112.7 1.2 copy.4843
  113.9 47.4 %all-to-all-start = ((f32[1,3,256,128]{3,0,1,2:T(1,128)}), f32[1,3,256,128]{3,0,1,2:T(1,128)S(1)}, u32[]{:S(2)}, u32[]{:S(2)}) async-start(f32[1,3,256,128]{3,0,1,2:T(1,128)} %copy.4843), calls=%async_computation | async-start | bytes 786432 | tf_op jit(solution)/shard_map/all_to_all | solution.py:171
  161.3 0.6 copy-done.3
  162.0 0.6 copy-done.4
  162.6 23.9 %all-to-all-done = f32[1,3,256,128]{3,0,1,2:T(1,128)S(1)} async-done(((f32[1,3,256,128]{3,0,1,2:T(1,128)}), f32[1,3,256,128]{3,0,1,2:T(1,128)S(1)}, u32[]{:S(2)}, u32[]{:S(2)}) %all-to-all-start) | async-done | bytes 393248 | tf_op jit(solution)/shard_map/all_to_all | solution.py:171
  186.7 0.6 gather_fusion
  187.5 0.6 copy-done.2
  188.2 2.6 collective-permute-start.6
  190.8 13.5 %collective-permute-start.7 = (f32[3,128]{1,0:T(4,128)S(1)}, f32[3,128]{1,0:T(4,128)S(1)}, u32[]{:S(2)}, u32[]{:S(2)}) collective-permute-start(f32[3,128]{1,0:T(4,128)S(1)} %pad_maximum_fusion.27), channel_id=1, source_target_pairs={{0,508},{4,0},{8,4},{12,8},{16,12},{20,16},{24,20},{28,24},{32,28}... | collective-permute-start | bytes 4616 | tf_op jit(solution)/shard_map/ppermute | solution.py:37
  204.3 1.9 collective-permute-start.8
  206.2 13.3 %collective-permute-start.9 = (f32[3,128]{1,0:T(4,128)S(1)}, f32[3,128]{1,0:T(4,128)S(1)}, u32[]{:S(2)}, u32[]{:S(2)}) collective-permute-start(f32[3,128]{1,0:T(4,128)S(1)} %pad_maximum_fusion.27), channel_id=1, source_target_pairs={{0,504},{4,508},{8,0},{12,4},{16,8},{20,12},{24,16},{28,20},{32,24... | collective-permute-start | bytes 4616 | tf_op jit(solution)/shard_map/ppermute | solution.py:37
  219.5 1.9 collective-permute-start.2
  221.5 14.2 %collective-permute-start.3 = (f32[128,128]{1,0:T(8,128)S(1)}, f32[128,128]{1,0:T(8,128)S(1)}, u32[]{:S(2)}, u32[]{:S(2)}) collective-permute-start(f32[128,128]{1,0:T(8,128)S(1)} %get-tuple-element.38), channel_id=1, source_target_pairs={{0,508},{4,0},{8,4},{12,8},{16,12},{20,16},{24,20},{28,24},{32,28}... | collective-permute-start | bytes 196616 | tf_op jit(solution)/shard_map/ppermute | solution.py:37
  235.7 1.9 collective-permute-start.4
  237.7 13.3 %collective-permute-start.5 = (f32[128,128]{1,0:T(8,128)S(1)}, f32[128,128]{1,0:T(8,128)S(1)}, u32[]{:S(2)}, u32[]{:S(2)}) collective-permute-start(f32[128,128]{1,0:T(8,128)S(1)} %get-tuple-element.38), channel_id=1, source_target_pairs={{0,504},{4,508},{8,0},{12,4},{16,8},{20,12},{24,16},{28,20},{32,24... | collective-permute-start | bytes 196616 | tf_op jit(solution)/shard_map/ppermute | solution.py:37
  251.2 1.1 collective-permute-done.5
  252.3 0.7 fusion.36
  253.0 0.6 fusion.34
  253.7 1.1 broadcast_in_dim.31
  254.8 20.6 %all-to-all-start.1 = ((f32[4,1,33024]{2,1,0:T(1,128)}), f32[4,1,33024]{2,1,0:T(1,128)S(1)}, u32[]{:S(2)}, u32[]{:S(2)}) async-start(f32[4,1,33024]{2,1,0:T(1,128)} %broadcast_in_dim.31), calls=%async_computation.1 | async-start | bytes 1056768 | tf_op jit(solution)/shard_map/all_to_all | solution.py:42
  275.6 16.4 %all-to-all-done.1 = f32[4,1,33024]{2,1,0:T(1,128)S(1)} async-done(((f32[4,1,33024]{2,1,0:T(1,128)}), f32[4,1,33024]{2,1,0:T(1,128)S(1)}, u32[]{:S(2)}, u32[]{:S(2)}) %all-to-all-start.1) | async-done | bytes 528416 | tf_op jit(solution)/shard_map/all_to_all | solution.py:42
  292.0 0.5 reduce_sum.39
  299.1 0.7 slice-done
  300.4 0.6 fusion.25
  303.4 40.8 %all_to_all.29 = f32[128,1,3,2,128]{4,3,2,1,0:T(2,128)S(1)} all-to-all(f32[128,1,3,2,128]{4,3,2,1,0:T(2,128)S(1)} %copy.4913), channel_id=1, replica_groups=mesh['mem'=128,'slab'=4] {'mem'}, dimensions={0} | all-to-all | bytes 786432 | tf_op jit(solution)/shard_map/all_to_all | solution.py:202
  344.3 0.8 copy.4915
  (351 shorter events, 27.9 us)
Async XLA Ops:
  0.0 1.0 copy-start
  1.2 22.6 %collective-permute-start = (f32[3,256,4]{2,1,0:T(8,128)S(1)}, f32[3,256,4]{2,1,0:T(8,128)S(1)}, u32[]{:S(2)}, u32[]{:S(2)}) collective-permute-start(f32[3,256,4]{2,1,0:T(8,128)S(1)} %get-tuple-element.391), channel_id=1, source_target_pairs={{1,0},{2,1},{3,2},{0,3},{5,4},{6,5},{7,6},{4,7},{9,8},{10,9},{11,1... | collective-permute-start | bytes 36872 | tf_op jit(solution)/shard_map/while/body/eval_jaxpr/ppermute | solution.py:27
  9.9 32.1 %collective-permute-start.1 = (f32[3,256,4]{2,1,0:T(8,128)S(1)}, f32[3,256,4]{2,1,0:T(8,128)S(1)}, u32[]{:S(2)}, u32[]{:S(2)}) collective-permute-start(f32[3,256,4]{2,1,0:T(8,128)S(1)} %get-tuple-element.392), channel_id=1, source_target_pairs={{0,1},{1,2},{2,3},{3,0},{4,5},{5,6},{6,7},{7,4},{8,9},{9,10},{10,1... | collective-permute-start | bytes 36872 | tf_op jit(solution)/shard_map/while/body/eval_jaxpr/ppermute | solution.py:25
  50.1 27.0 %collective-permute-start = (f32[3,256,4]{2,1,0:T(8,128)S(1)}, f32[3,256,4]{2,1,0:T(8,128)S(1)}, u32[]{:S(2)}, u32[]{:S(2)}) collective-permute-start(f32[3,256,4]{2,1,0:T(8,128)S(1)} %get-tuple-element.391), channel_id=1, source_target_pairs={{1,0},{2,1},{3,2},{0,3},{5,4},{6,5},{7,6},{4,7},{9,8},{10,9},{11,1... | collective-permute-start | bytes 36872 | tf_op jit(solution)/shard_map/while/body/eval_jaxpr/ppermute | solution.py:27
  53.4 23.7 %collective-permute-start.1 = (f32[3,256,4]{2,1,0:T(8,128)S(1)}, f32[3,256,4]{2,1,0:T(8,128)S(1)}, u32[]{:S(2)}, u32[]{:S(2)}) collective-permute-start(f32[3,256,4]{2,1,0:T(8,128)S(1)} %get-tuple-element.392), channel_id=1, source_target_pairs={{0,1},{1,2},{2,3},{3,0},{4,5},{5,6},{6,7},{7,4},{8,9},{9,10},{10,1... | collective-permute-start | bytes 36872 | tf_op jit(solution)/shard_map/while/body/eval_jaxpr/ppermute | solution.py:25
  85.2 19.6 %collective-permute-start = (f32[3,256,4]{2,1,0:T(8,128)S(1)}, f32[3,256,4]{2,1,0:T(8,128)S(1)}, u32[]{:S(2)}, u32[]{:S(2)}) collective-permute-start(f32[3,256,4]{2,1,0:T(8,128)S(1)} %get-tuple-element.391), channel_id=1, source_target_pairs={{1,0},{2,1},{3,2},{0,3},{5,4},{6,5},{7,6},{4,7},{9,8},{10,9},{11,1... | collective-permute-start | bytes 36872 | tf_op jit(solution)/shard_map/while/body/eval_jaxpr/ppermute | solution.py:27
  90.3 14.5 %collective-permute-start.1 = (f32[3,256,4]{2,1,0:T(8,128)S(1)}, f32[3,256,4]{2,1,0:T(8,128)S(1)}, u32[]{:S(2)}, u32[]{:S(2)}) collective-permute-start(f32[3,256,4]{2,1,0:T(8,128)S(1)} %get-tuple-element.392), channel_id=1, source_target_pairs={{0,1},{1,2},{2,3},{3,0},{4,5},{5,6},{6,7},{7,4},{8,9},{9,10},{10,1... | collective-permute-start | bytes 36872 | tf_op jit(solution)/shard_map/while/body/eval_jaxpr/ppermute | solution.py:25
  113.9 72.7 %all-to-all-start = ((f32[1,3,256,128]{3,0,1,2:T(1,128)}), f32[1,3,256,128]{3,0,1,2:T(1,128)S(1)}, u32[]{:S(2)}, u32[]{:S(2)}) async-start(f32[1,3,256,128]{3,0,1,2:T(1,128)} %copy.4843), calls=%async_computation | async-start | bytes 786432 | tf_op jit(solution)/shard_map/all_to_all | solution.py:171
  161.3 0.7 copy-start.3
  162.0 0.7 copy-start.4
  187.5 0.7 copy-start.2
  188.2 33.3 %collective-permute-start.6 = (f32[3,128]{1,0:T(4,128)S(1)}, f32[3,128]{1,0:T(4,128)S(1)}, u32[]{:S(2)}, u32[]{:S(2)}) collective-permute-start(f32[3,128]{1,0:T(4,128)S(1)} %pad_maximum_fusion.27), channel_id=1, source_target_pairs={{0,4},{4,8},{8,12},{12,16},{16,20},{20,24},{24,28},{28,32},{32,36}... | collective-permute-start | bytes 4616 | tf_op jit(solution)/shard_map/ppermute | solution.py:37
  190.8 44.9 %collective-permute-start.7 = (f32[3,128]{1,0:T(4,128)S(1)}, f32[3,128]{1,0:T(4,128)S(1)}, u32[]{:S(2)}, u32[]{:S(2)}) collective-permute-start(f32[3,128]{1,0:T(4,128)S(1)} %pad_maximum_fusion.27), channel_id=1, source_target_pairs={{0,508},{4,0},{8,4},{12,8},{16,12},{20,16},{24,20},{28,24},{32,28}... | collective-permute-start | bytes 4616 | tf_op jit(solution)/shard_map/ppermute | solution.py:37
  204.3 33.4 %collective-permute-start.8 = (f32[3,128]{1,0:T(4,128)S(1)}, f32[3,128]{1,0:T(4,128)S(1)}, u32[]{:S(2)}, u32[]{:S(2)}) collective-permute-start(f32[3,128]{1,0:T(4,128)S(1)} %pad_maximum_fusion.27), channel_id=1, source_target_pairs={{0,8},{4,12},{8,16},{12,20},{16,24},{20,28},{24,32},{28,36},{32,40... | collective-permute-start | bytes 4616 | tf_op jit(solution)/shard_map/ppermute | solution.py:37
  206.2 44.8 %collective-permute-start.9 = (f32[3,128]{1,0:T(4,128)S(1)}, f32[3,128]{1,0:T(4,128)S(1)}, u32[]{:S(2)}, u32[]{:S(2)}) collective-permute-start(f32[3,128]{1,0:T(4,128)S(1)} %pad_maximum_fusion.27), channel_id=1, source_target_pairs={{0,504},{4,508},{8,0},{12,4},{16,8},{20,12},{24,16},{28,20},{32,24... | collective-permute-start | bytes 4616 | tf_op jit(solution)/shard_map/ppermute | solution.py:37
  219.5 31.6 %collective-permute-start.2 = (f32[128,128]{1,0:T(8,128)S(1)}, f32[128,128]{1,0:T(8,128)S(1)}, u32[]{:S(2)}, u32[]{:S(2)}) collective-permute-start(f32[128,128]{1,0:T(8,128)S(1)} %get-tuple-element.38), channel_id=1, source_target_pairs={{0,4},{4,8},{8,12},{12,16},{16,20},{20,24},{24,28},{28,32},{32,36}... | collective-permute-start | bytes 196616 | tf_op jit(solution)/shard_map/ppermute | solution.py:37
  221.5 29.6 %collective-permute-start.3 = (f32[128,128]{1,0:T(8,128)S(1)}, f32[128,128]{1,0:T(8,128)S(1)}, u32[]{:S(2)}, u32[]{:S(2)}) collective-permute-start(f32[128,128]{1,0:T(8,128)S(1)} %get-tuple-element.38), channel_id=1, source_target_pairs={{0,508},{4,0},{8,4},{12,8},{16,12},{20,16},{24,20},{28,24},{32,28}... | collective-permute-start | bytes 196616 | tf_op jit(solution)/shard_map/ppermute | solution.py:37
  235.7 15.5 %collective-permute-start.4 = (f32[128,128]{1,0:T(8,128)S(1)}, f32[128,128]{1,0:T(8,128)S(1)}, u32[]{:S(2)}, u32[]{:S(2)}) collective-permute-start(f32[128,128]{1,0:T(8,128)S(1)} %get-tuple-element.38), channel_id=1, source_target_pairs={{0,8},{4,12},{8,16},{12,20},{16,24},{20,28},{24,32},{28,36},{32,40... | collective-permute-start | bytes 196616 | tf_op jit(solution)/shard_map/ppermute | solution.py:37
  237.7 14.6 %collective-permute-start.5 = (f32[128,128]{1,0:T(8,128)S(1)}, f32[128,128]{1,0:T(8,128)S(1)}, u32[]{:S(2)}, u32[]{:S(2)}) collective-permute-start(f32[128,128]{1,0:T(8,128)S(1)} %get-tuple-element.38), channel_id=1, source_target_pairs={{0,504},{4,508},{8,0},{12,4},{16,8},{20,12},{24,16},{28,20},{32,24... | collective-permute-start | bytes 196616 | tf_op jit(solution)/shard_map/ppermute | solution.py:37
  254.8 37.2 %all-to-all-start.1 = ((f32[4,1,33024]{2,1,0:T(1,128)}), f32[4,1,33024]{2,1,0:T(1,128)S(1)}, u32[]{:S(2)}, u32[]{:S(2)}) async-start(f32[4,1,33024]{2,1,0:T(1,128)} %broadcast_in_dim.31), calls=%async_computation.1 | async-start | bytes 1056768 | tf_op jit(solution)/shard_map/all_to_all | solution.py:42
  292.5 6.1 %copy-start.1 = (f32[33024]{0:T(1024)}, f32[33024]{0:T(1024)S(1)}, u32[]{:S(2)}) copy-start(f32[33024]{0:T(1024)S(1)} %reduce_sum.39) | copy-start | bytes 396292
  299.1 0.7 slice-start
